TPU v7x, 32 devices: a whole 2x2x4 slice. The times are simulated.
32 devices in a mesh: expert: 8 (over z, x), mp: 4 (over y, core).
Axes of the slice: x: 2, y: 2, z: 4, core: 2. Of those that a mesh axis runs over, the one named last changes fastest.
Arguments:
- tokens: bfloat16 [192, 6144], P('expert', 'mp'), may hold values from -6 to 6
- mix_weights: float32 [192, 2], P('expert'), may hold values from 0.2 to 1
- routes: int32 [192, 2], P('expert'), may hold values from 0 to 7, as said below
- w_gate: bfloat16 [8, 6144, 8192], P('expert', None, 'mp'), may hold values from -0.078125 to 0.078125
- w_up: bfloat16 [8, 6144, 8192], P('expert', None, 'mp'), may hold values from -0.078125 to 0.078125
- w_down: bfloat16 [8, 8192, 6144], P('expert', 'mp'), may hold values from -0.0625 to 0.0625
Outputs:
- mixed_out: bfloat16 [192, 6144], P('expert', 'mp')
Inputs may be any that keep to these rules, and one draw needn't show every extreme that they name: `routes`: each row names 2 different experts, and every expert is named by some row. Among the 24 rows of one index of the expert axis no expert is named more than 12 times, and on some indices one is named exactly 12 times.
All inputs are finite; a program needn't handle non-finite values.
Results may differ from a plain program's by a relative error of at most 0.011.
Values may be sent and summed in bfloat16 or wider, within the bound.
A program may use at most 128 MiB of HBM per device.

v0:
```python
import functools

import jax
import jax.numpy as jnp
from jax import lax
from jax.experimental import pallas as pl
from jax.experimental.pallas import tpu as pltpu
from jax.sharding import PartitionSpec as P

EXPERTS = 8
TOP = 2
BLOCK = 16
LANES = 128
COLS = 256
MESH = pl.DeviceIdType.MESH


def fused(
    senders, capacity,
    tokens, mix, routes, w_gate, w_up, w_down, out,
    wbuf, packed, arrived, x, hidden, acc, cnt_send, cnt_all, pick_w, compact,
    own, red_send, red_recv, ret_send, ret_recv,
    w_sem, d_sem, cs_sem, cr_sem, as_sem, ar_sem, ys_sem, yr_sem, ss_sem, sr_sem,
    rs_sem, rr_sem, ts_sem, tr_sem,
):
    me = lax.axis_index("expert")
    m = lax.axis_index("mp")
    sibling = m + 1 - 2 * lax.rem(m, 2)
    across = lax.rem(m + 2, 4)
    across_sibling = lax.rem(sibling + 2, 4)
    tok_rows = tokens.shape[0]
    depth, units = w_gate.shape[1], w_gate.shape[2] // COLS
    ff = w_down.shape[1]
    fit = depth // ff
    pieces = depth // COLS
    rounds = pieces // 4
    width = tokens.shape[1]
    slots = x.shape[0]

    def peer(d):
        return lax.rem(me + d, senders)

    def from_peer(d):
        return lax.rem(me + senders - d, senders)

    def remote(src, dst, send, recv, to_expert, to_mp):
        return pltpu.make_async_remote_copy(
            src_ref=src, dst_ref=dst, send_sem=send, recv_sem=recv,
            device_id=(to_expert, to_mp), device_id_type=MESH,
        )

    order = (m, sibling, across, across_sibling)

    def weight_copy(src, half, q, n):
        rows = pl.ds(pl.multiple_of(order[q] * width, width), width)
        return pltpu.make_async_copy(
            src.at[0, rows, pl.ds(pl.multiple_of(n * COLS, COLS), COLS)],
            wbuf.at[n, rows, pl.ds(half * COLS, COLS)],
            w_sem.at[q, half, n],
        )

    def pair_rows(t):
        return pl.ds(pl.multiple_of(lax.rem(t, fit) * ff, ff), ff)

    def piece_copy(t, half, j):
        c = t // 2
        owner = lax.rem(m + 1 + j, 4)
        start = pl.multiple_of(owner * width + c * COLS, COLS)
        return pltpu.make_async_copy(
            w_down.at[0, :, pl.ds(start, COLS)],
            wbuf.at[t // fit, pair_rows(t), pl.ds(half * COLS, COLS)],
            d_sem.at[t, half],
        )

    def prefetch(q):
        def body(n, carry):
            weight_copy(w_gate, 0, q, n).start()
            weight_copy(w_up, 1, q, n).start()
            return carry

        lax.fori_loop(0, units, body, 0)

    barrier = pltpu.get_barrier_semaphore()
    for d in range(1, senders):
        pl.semaphore_signal(barrier, inc=1, device_id=(peer(d), m), device_id_type=MESH)
    for d in range(1, 4):
        pl.semaphore_signal(
            barrier, inc=1, device_id=(me, lax.rem(m + d, 4)), device_id_type=MESH
        )
    for q in range(4):
        prefetch(q)

    lane = lax.broadcasted_iota(jnp.int32, (tok_rows, LANES), 1)
    lane_expert, lane_rank = lane // BLOCK, lax.rem(lane, BLOCK)
    ids = routes[...]
    first = jnp.where(ids[:, 0:1] == lane_expert, 1.0, 0.0)
    second = jnp.where(ids[:, 1:2] == lane_expert, 1.0, 0.0)
    marked = first + second
    row_at = lax.broadcasted_iota(jnp.int32, (tok_rows, tok_rows), 0)
    col_at = lax.broadcasted_iota(jnp.int32, (tok_rows, tok_rows), 1)
    below = jnp.where(col_at < row_at, 1.0, 0.0).astype(jnp.bfloat16)
    earlier = jnp.dot(below, marked.astype(jnp.bfloat16), preferred_element_type=jnp.float32)
    pick = marked * jnp.where(earlier == lane_rank.astype(jnp.float32), 1.0, 0.0)
    cnt_send[...] = jnp.broadcast_to(jnp.sum(marked, axis=0, keepdims=True), cnt_send.shape)
    blocks = lax.dot_general(
        pick.astype(jnp.bfloat16), tokens[...], (((0,), (0,)), ((), ())),
        preferred_element_type=jnp.float32,
    ).astype(jnp.bfloat16).reshape(packed.shape)
    packed[...] = blocks
    arrived[m, me] = packed[me]
    cnt_all[me] = cnt_send[...]

    pl.semaphore_wait(barrier, senders - 1 + 3)

    def block_copy(d):
        return remote(packed.at[peer(d)], arrived.at[m, me], as_sem.at[d - 1], ar_sem.at[d - 1], peer(d), m)

    def count_copy(d):
        return remote(cnt_send, cnt_all.at[me], cs_sem.at[d - 1], cr_sem.at[d - 1], peer(d), m)

    def across_copy(d):
        block = arrived.at[m, from_peer(d)]
        return remote(block, block, ys_sem.at[d], yr_sem.at[d], me, across)

    def sibling_copy(d, which, at):
        block = arrived.at[which, from_peer(d)]
        return remote(block, block, ss_sem.at[at, d], sr_sem.at[at, d], me, sibling)

    for d in range(1, senders):
        block_copy(d).start()
    for d in range(1, senders):
        count_copy(d).start()
    for d in range(senders):
        if d:
            block_copy(d).wait_recv()
        across_copy(d).start()
        sibling_copy(d, m, 0).start()
    for d in range(1, senders):
        count_copy(d).wait_recv()

    counts = cnt_all[:, 0, :]
    expert_lane = lax.broadcasted_iota(jnp.int32, (senders, LANES), 1)
    sender_row = lax.broadcasted_iota(jnp.int32, (senders, LANES), 0)
    mine = jnp.sum(jnp.where(expert_lane == me * BLOCK, counts, 0.0), axis=1, keepdims=True)
    block_of = expert_lane // BLOCK
    lane_cnt = jnp.sum(jnp.where(block_of == sender_row, mine, 0.0), axis=0, keepdims=True)
    lane_off = jnp.sum(jnp.where(sender_row < block_of, mine, 0.0), axis=0, keepdims=True)
    rank_f = lax.rem(lax.broadcasted_iota(jnp.int32, (slots, LANES), 1), BLOCK).astype(jnp.float32)
    slot_f = lax.broadcasted_iota(jnp.int32, (slots, LANES), 0).astype(jnp.float32)
    hit = jnp.where(rank_f < lane_cnt, 1.0, 0.0) * jnp.where(rank_f + lane_off == slot_f, 1.0, 0.0)
    hit = hit * jnp.where(slot_f < capacity, 1.0, 0.0)
    compact[...] = hit.astype(jnp.bfloat16)

    offset = jnp.sum(jnp.where(sender_row < me, counts, 0.0), axis=0, keepdims=True)
    weights = mix[...]
    weighted = pick * (first * weights[:, 0:1] + second * weights[:, 1:2])
    weighted = weighted * jnp.where(offset + earlier < capacity, 1.0, 0.0)
    high = weighted.astype(jnp.bfloat16)
    pick_w[0] = high
    pick_w[1] = (weighted - high.astype(jnp.float32)).astype(jnp.bfloat16)

    def gather(which):
        rows = arrived[which].reshape(senders * BLOCK, width)
        got = jnp.dot(compact[...], rows, preferred_element_type=jnp.float32)
        x[:, pl.ds(pl.multiple_of(which * width, width), width)] = got.astype(jnp.bfloat16)

    def partial(q, n):
        weight_copy(w_gate, 0, q, n).wait()
        weight_copy(w_up, 1, q, n).wait()
        rows = pl.ds(pl.multiple_of(order[q] * width, width), width)
        return jnp.dot(x[:, rows], wbuf[n, rows, :], preferred_element_type=jnp.float32)

    def opening(n, carry):
        acc[n] = partial(0, n)
        return carry

    def adding(q):
        def body(n, carry):
            acc[n] = acc[n] + partial(q, n)
            return carry

        lax.fori_loop(0, units, body, 0)

    def closing(n, carry):
        both = acc[n] + partial(3, n)
        gate, up = both[:, :COLS], both[:, COLS:]
        act = gate / (1.0 + jnp.exp(-gate)) * up
        hidden[:, pl.ds(pl.multiple_of(n * COLS, COLS), COLS)] = act.astype(jnp.bfloat16)

        @pl.when(n < pieces // (2 * fit))
        def _():
            for i in range(fit):
                t = n * fit + i
                for half in range(2):
                    piece_copy(t, half, 2 * lax.rem(t, 2) + half).start()

        return carry

    gather(m)
    lax.fori_loop(0, units, opening, 0)
    for d in range(senders):
        sibling_copy(d, m, 0).wait_recv()
    gather(sibling)
    adding(1)
    for d in range(senders):
        across_copy(d).wait_recv()
        sibling_copy(d, across, 1).start()
    gather(across)
    adding(2)
    for d in range(senders):
        sibling_copy(d, across, 1).wait_recv()
    gather(across_sibling)
    lax.fori_loop(0, units, closing, 0)

    def reduce_copy(c, j):
        owner = lax.rem(m + 1 + j, 4)
        return remote(red_send.at[c, j], red_recv.at[c, j], rs_sem.at[c, j], rr_sem.at[c, j], me, owner)

    def return_copy(c, d):
        return remote(ret_send.at[c, peer(d)], ret_recv.at[c, me], ts_sem.at[c, d - 1], tr_sem.at[c, d - 1], peer(d), m)

    def send_back(c):
        total = own[c]
        for j in range(3):
            reduce_copy(c, j).wait_recv()
            total = total + red_recv[c, j].astype(jnp.float32)
        spread = lax.dot_general(
            compact[...], total.astype(jnp.bfloat16), (((0,), (0,)), ((), ())),
            preferred_element_type=jnp.float32,
        ).astype(jnp.bfloat16)
        ret_send[c] = spread.reshape(senders, BLOCK, COLS)
        ret_recv[c, me] = ret_send[c, me]
        for d in range(1, senders):
            return_copy(c, d).start()

    lag = 2

    def down(c, carry):
        for i in range(2):
            t = c * 2 + i
            piece_copy(t, 0, 2 * i).wait()
            piece_copy(t, 1, 2 * i + 1).wait()
            part = jnp.dot(
                hidden[...], wbuf[t // fit, pair_rows(t), :], preferred_element_type=jnp.float32
            )
            for half in range(2):
                j = 2 * i + half
                piece = part[:, half * COLS : (half + 1) * COLS]
                if j < 3:
                    red_send[c, j] = piece.astype(jnp.bfloat16)
                    reduce_copy(c, j).start()
                else:
                    own[c] = piece

        @pl.when(c >= lag)
        def _():
            send_back(c - lag)

        return carry

    lax.fori_loop(0, rounds, down, 0)

    def last(c, carry):
        send_back(c)
        return carry

    lax.fori_loop(rounds - lag, rounds, last, 0)

    def combine(c, carry):
        for d in range(1, senders):
            return_copy(c, d).wait_recv()
        rows = ret_recv[c].reshape(LANES, COLS)
        mixed = jnp.dot(pick_w[0], rows, preferred_element_type=jnp.float32)
        mixed = mixed + jnp.dot(pick_w[1], rows, preferred_element_type=jnp.float32)
        out[:, pl.ds(pl.multiple_of(c * COLS, COLS), COLS)] = mixed.astype(jnp.bfloat16)
        return carry

    lax.fori_loop(0, rounds, combine, 0)

    for d in range(1, senders):
        block_copy(d).wait_send()
        count_copy(d).wait_send()
    for d in range(senders):
        across_copy(d).wait_send()
        sibling_copy(d, m, 0).wait_send()
        sibling_copy(d, across, 1).wait_send()

    def drain(c, carry):
        for j in range(3):
            reduce_copy(c, j).wait_send()
        for d in range(1, senders):
            return_copy(c, d).wait_send()
        return carry

    lax.fori_loop(0, rounds, drain, 0)


def local_fused(tokens, mix_weights, routes, w_gate, w_up, w_down):
    tok_rows, width = tokens.shape
    senders = lax.axis_size("expert")
    capacity = 5 * tok_rows * senders * TOP // (4 * EXPERTS)
    slots = -(-capacity // BLOCK) * BLOCK
    depth, ff = w_gate.shape[1], w_gate.shape[2]
    units = ff // COLS
    pieces = depth // COLS
    rounds = pieces // 4
    bf16, f32 = jnp.bfloat16, jnp.float32
    dma = pltpu.SemaphoreType.DMA
    vmem = pl.BlockSpec(memory_space=pltpu.VMEM)
    hbm = pl.BlockSpec(memory_space=pl.ANY)
    return pl.pallas_call(
        functools.partial(fused, senders, capacity),
        out_shape=jax.ShapeDtypeStruct((tok_rows, width), bf16),
        in_specs=[vmem, vmem, vmem, hbm, hbm, hbm],
        out_specs=vmem,
        scratch_shapes=[
            pltpu.VMEM((units, depth, 2 * COLS), bf16),
            pltpu.VMEM((senders, BLOCK, width), bf16),
            pltpu.VMEM((4, senders, BLOCK, width), bf16),
            pltpu.VMEM((slots, depth), bf16),
            pltpu.VMEM((slots, ff), bf16),
            pltpu.VMEM((units, slots, 2 * COLS), f32),
            pltpu.VMEM((8, LANES), f32),
            pltpu.VMEM((senders, 8, LANES), f32),
            pltpu.VMEM((2, tok_rows, LANES), bf16),
            pltpu.VMEM((slots, LANES), bf16),
            pltpu.VMEM((rounds, slots, COLS), f32),
            pltpu.VMEM((rounds, 3, slots, COLS), bf16),
            pltpu.VMEM((rounds, 3, slots, COLS), bf16),
            pltpu.VMEM((rounds, senders, BLOCK, COLS), bf16),
            pltpu.VMEM((rounds, senders, BLOCK, COLS), bf16),
            dma((4, 2, units)),
            dma((pieces // 2, 2)),
            dma((senders - 1,)),
            dma((senders - 1,)),
            dma((senders - 1,)),
            dma((senders - 1,)),
            dma((senders,)),
            dma((senders,)),
            dma((2, senders)),
            dma((2, senders)),
            dma((rounds, 3)),
            dma((rounds, 3)),
            dma((rounds, senders - 1)),
            dma((rounds, senders - 1)),
        ],
        compiler_params=pltpu.CompilerParams(
            collective_id=0, has_side_effects=True, vmem_limit_bytes=67_043_328
        ),
    )(tokens, mix_weights, routes, w_gate, w_up, w_down)


def fits(tokens, w_gate):
    senders, ways = lax.axis_size("expert"), lax.axis_size("mp")
    tok_rows, width = tokens.shape
    depth, ff = w_gate.shape[1], w_gate.shape[2]
    return (
        senders == EXPERTS
        and senders * BLOCK == LANES
        and ways == 4
        and tok_rows // 2 <= BLOCK
        and tok_rows % 8 == 0
        and width % COLS == 0
        and ff % COLS == 0
        and depth % ff == 0
        and (depth // COLS) % (2 * (depth // ff)) == 0
        and depth // COLS <= 2 * (ff // COLS) * (depth // ff)
        and width // COLS > 2
        and 4 * depth * ff <= 52 * 2**20
    )


def local_any(tokens, mix_weights, routes, w_gate, w_up, w_down):
    form = local_fused if fits(tokens, w_gate) else local
    return form(tokens, mix_weights, routes, w_gate, w_up, w_down)


def pack_rows(pick_tokens, features, repeats):
    packed = jnp.einsum(
        "tem,tc->emc", pick_tokens, features, preferred_element_type=jnp.float32
    ).astype(jnp.bfloat16)
    spread = jnp.broadcast_to(packed[:, None], (packed.shape[0], repeats) + packed.shape[1:])
    return spread.reshape((packed.shape[0] * repeats,) + packed.shape[1:])


def activate(gate_act, up_act):
    return (jax.nn.silu(gate_act) * up_act).astype(jnp.bfloat16)


def local(tokens, mix_weights, routes, w_gate, w_up, w_down):
    tok_rows = tokens.shape[0]
    senders = lax.axis_size("expert")
    group_size = senders // EXPERTS
    capacity = 5 * tok_rows * senders * TOP // (4 * EXPERTS)
    most_rows = tok_rows // 2
    labels = jnp.arange(EXPERTS, dtype=jnp.int32)
    flat_ids = routes.reshape(-1)
    marked = (flat_ids[:, None] == labels[None, :]).astype(jnp.int32)
    earlier = jnp.cumsum(marked, axis=0) - marked
    local_rank = jnp.sum(earlier * marked, axis=1)
    counts = jnp.sum(marked, axis=0)
    count_grid = lax.all_gather(counts[None, :], "expert", axis=0, tiled=True)
    my_index = lax.axis_index("expert")
    sender_ids = jnp.arange(senders, dtype=jnp.int32)
    lower_mask = (sender_ids[:, None] < my_index).astype(jnp.int32)
    offsets = jnp.sum(count_grid * lower_mask, axis=0)
    slot_ids = jnp.sum(marked * offsets[None, :], axis=1) + local_rank
    keep_mask = (slot_ids < capacity).astype(jnp.int32)
    rank_hit = (local_rank[:, None] == jnp.arange(most_rows, dtype=jnp.int32)[None, :]).astype(
        jnp.int32
    ) * keep_mask[:, None]
    assign_pick = marked[:, :, None] * rank_hit[:, None, :]
    pick_tokens = jnp.sum(assign_pick.reshape(tok_rows, TOP, EXPERTS, most_rows), axis=1).astype(
        jnp.bfloat16
    )
    weighted = assign_pick.astype(jnp.float32) * mix_weights.reshape(-1)[:, None, None]
    combine_w = jnp.sum(weighted.reshape(tok_rows, TOP, EXPERTS * most_rows), axis=1)
    gate_rows = w_gate[0]
    up_rows = w_up[0]
    down_rows = w_down[0]
    arrived = lax.all_to_all(
        pack_rows(pick_tokens, tokens, group_size),
        "expert",
        split_axis=0,
        concat_axis=0,
        tiled=True,
    )
    arrived_rows = arrived.reshape(senders * most_rows, arrived.shape[2])
    shard_piece = lax.all_gather(arrived_rows, "mp", axis=1, tiled=True)
    gate_act = jnp.dot(shard_piece, gate_rows, preferred_element_type=jnp.float32)
    up_act = jnp.dot(shard_piece, up_rows, preferred_element_type=jnp.float32)
    hidden = activate(gate_act, up_act)
    part_sum = jnp.dot(hidden, down_rows, preferred_element_type=jnp.float32)
    reduced = lax.psum_scatter(part_sum, "mp", scatter_dimension=1, tiled=True).astype(jnp.bfloat16)
    out_width = reduced.shape[1]
    returned = lax.all_to_all(
        reduced.reshape(senders, most_rows, out_width),
        "expert",
        split_axis=0,
        concat_axis=0,
        tiled=True,
    )
    summed = jnp.sum(
        returned.reshape(EXPERTS, group_size, most_rows, out_width).astype(jnp.float32), axis=1
    )
    result = jnp.dot(
        combine_w, summed.reshape(EXPERTS * most_rows, out_width), precision=lax.Precision.HIGHEST
    )
    return result.astype(jnp.bfloat16)


def solution(mesh):
    placed = (
        P("expert", "mp"),
        P("expert", None),
        P("expert", None),
        P("expert", None, "mp"),
        P("expert", None, "mp"),
        P("expert", "mp", None),
    )
    return jax.shard_map(
        local_any, mesh=mesh, in_specs=placed, out_specs=P("expert", "mp"), check_vma=False
    )
```

profile of v0, /device:TPU:0, one launch (start us, length us, event | category | flops | bytes accessed | tf_op | source)
XLA Modules:
  0.0 54.6 jit_solution(13670120765708849260)
XLA Ops:
  0.0 1.4 %copy.7.mix = f32[24,2]{1,0:T(8,128)} copy(f32[24,2]{0,1:T(2,128)} %param.7) | data formatting | bytes 384 | tf_op args[1]
  1.4 1.4 %copy.8.routes = s32[24,2]{1,0:T(8,128)} copy(s32[24,2]{0,1:T(2,128)} %param.8) | data formatting | bytes 384 | tf_op args[2]
  2.7 50.3 %shard_map.64 = bf16[24,1536]{1,0:T(8,128)(2,1)} custom-call(bf16[24,1536]{1,0:T(8,128)(2,1)} %tokens.1, f32[24,2]{1,0:T(8,128)} %copy.7.mix, s32[24,2]{1,0:T(8,128)} %copy.8.routes, bf16[1,6144,2048]{2,1,0:T(8,128)(2,1)} %w_gate.1, bf16[1,6144,2048]{2,1,0:T(8,128)(2,1)} %w_up.1, bf16[1,2048,6144]{2,1,0:T(8,128)(2,1)} %w_down.1), custom_call_target="tpu_custom_call" | custom-call | tf_op jit(solution)/shard_map/pallas_call | solution.py:311
  53.0 1.5 %copy.10 = bf16[24,1536]{1,0:T(8,128)(2,1)} copy(bf16[24,1536]{1,0:T(8,128)(2,1)} %shard_map.64) | data formatting | bytes 147456
where the time goes:
time: 54.8 us; the launch traced here: 54.6 us
  Pallas kernels  50.3 us (92%)
  local copies, waits for them, and re-layouts  4.23 us (8%)
    pallas_call x1, Pallas kernels, local_fused(): pl.pallas_call(functools.partial(fused, senders, capacity), out_shape=jax...  50.3 us
    unnamed x3, local copies, waits for them, and re-layouts  4.23 us

commit v1 on v0

v1 whole, which is shorter than its diff:
```python
import functools

import jax
import jax.numpy as jnp
from jax import lax
from jax.experimental import pallas as pl
from jax.experimental.pallas import tpu as pltpu
from jax.sharding import PartitionSpec as P

EXPERTS = 8
TOP = 2
STACK = 4
LANES = 128
SEG = STACK * LANES
TOKEN_PAD = 32
EXTRA = 4
ROUND_TO = 16
FAR_FIRST = (4, 3, 5, 2, 6, 1, 7)
MESH = pl.DeviceIdType.MESH
BF16, F32 = jnp.bfloat16, jnp.float32


def pass_order(chunks):
    arrival = (0, 12, 34, 45)
    pairs = [(which, c) for c in range(chunks) for which in range(4)]
    return sorted(pairs, key=lambda p: 21 * p[1] + arrival[p[0]])


def dot(a, b):
    return jnp.dot(a, b, preferred_element_type=F32)


def dot_nt(a, b):
    return lax.dot_general(a, b, (((1,), (1,)), ((), ())), preferred_element_type=F32)


def iota_f(shape, dim):
    return lax.broadcasted_iota(jnp.int32, shape, dim).astype(F32)


def split(index, size):
    high = jnp.floor((index + 0.5) * (1.0 / size))
    return high, index - high * size


def flag(cond):
    return jnp.where(cond, 1.0, 0.0)


def exchange(
    senders, capacity,
    tokens, mix, routes, w_gate, w_up, w_down, out,
    slots, tok, ids, mixw, packed, arrived, xbuf, acc, hidden, cnt_send, cnt_all,
    weighted, earlier_at, comp, spreader, weigh, own, pair_send, pair_recv,
    cross_send, cross_recv, ret_send, ret_recv,
):
    tok_rows, width = tokens.shape
    ff = w_gate.shape[2]
    chunks, cols_of = width // SEG, ff // SEG
    most = tok_rows // 2
    block = STACK * most
    stacked = senders * block
    n_slots = xbuf.shape[2]
    passes = pass_order(chunks)

    def body(
        w_sem, in_sem, cs_sem, cr_sem, as_sem, ar_sem, ss_sem, sr_sem, ys_sem, yr_sem,
        ps_sem, pr_sem, xs_sem, xr_sem, ts_sem, tr_sem,
    ):
        me = lax.axis_index("expert")
        m = lax.axis_index("mp")
        sibling = m + 1 - 2 * lax.rem(m, 2)
        across = lax.rem(m + 2, 4)
        across_sibling = lax.rem(sibling + 2, 4)
        order = (m, sibling, across, across_sibling)
        owners = (across_sibling, sibling, across, m)

        def peer(d):
            return lax.rem(me + d, senders)

        def remote(src, dst, send, recv, to_expert, to_mp):
            return pltpu.make_async_remote_copy(
                src_ref=src, dst_ref=dst, send_sem=send, recv_sem=recv,
                device_id=(to_expert, to_mp), device_id_type=MESH,
            )

        def weight_copy(i, up, b):
            which, c = passes[i]
            src = w_up if up else w_gate
            start = pl.multiple_of(order[which] * width + c * SEG, SEG)
            return pltpu.make_async_copy(
                src.at[0, pl.ds(start, SEG), pl.ds(b * SEG, SEG)],
                slots.at[2 * i + up, pl.ds(b * SEG, SEG), :],
                w_sem.at[2 * i + up, b],
            )

        def piece_slot(p):
            return 2 * len(passes) + p if p < EXTRA else p - EXTRA

        def piece_copy(p):
            start = pl.multiple_of(owners[p % 4] * width + (p // 4) * SEG, SEG)
            return pltpu.make_async_copy(
                w_down.at[0, :, pl.ds(start, SEG)], slots.at[piece_slot(p)], w_sem.at[piece_slot(p), 0]
            )

        barrier = pltpu.get_barrier_semaphore()
        for d in FAR_FIRST:
            pl.semaphore_signal(barrier, inc=1, device_id=(peer(d), m), device_id_type=MESH)
        for to in (across, across_sibling, sibling):
            pl.semaphore_signal(barrier, inc=1, device_id=(me, to), device_id_type=MESH)
        loads = (
            pltpu.make_async_copy(routes, ids, in_sem.at[0]),
            pltpu.make_async_copy(tokens, tok, in_sem.at[1]),
            pltpu.make_async_copy(mix, mixw, in_sem.at[2]),
        )
        for copy in loads:
            copy.start()
        for i in range(len(passes)):
            for up in range(2):
                for b in range(cols_of):
                    weight_copy(i, up, b).start(priority=1)
        for p in range(EXTRA):
            piece_copy(p).start(priority=1)

        row_e, row_rest = split(iota_f((stacked, tok_rows), 0), block)
        row_g, row_r = split(row_rest, most)
        upper = flag(iota_f((tok_rows, tok_rows), 0) < iota_f((tok_rows, tok_rows), 1)).astype(BF16)
        loads[0].wait()
        id_f = ids[...].astype(F32)
        first, second = flag(id_f[0:1, :] == row_e), flag(id_f[1:2, :] == row_e)
        marked = first + second
        earlier = dot(marked.astype(BF16), upper)
        sel = marked * flag(earlier == row_r)
        named = iota_f((LANES, tok_rows), 0)
        named = (flag(id_f[0:1, :] == named) + flag(id_f[1:2, :] == named)).astype(BF16)
        cnt_send[...] = dot_nt(jnp.ones((8, tok_rows), BF16), named)
        cnt_all[me] = cnt_send[...]
        loads[1].wait()
        loads[2].wait()
        total = None
        for j in range(STACK):
            segs = [tok[:, c * SEG + j * LANES : c * SEG + (j + 1) * LANES] for c in range(chunks)]
            part = dot((sel * flag(row_g == j)).astype(BF16), jnp.concatenate(segs, axis=1))
            total = part if total is None else total + part
        total = total.astype(BF16)
        for c in range(chunks):
            packed[c] = total[:, c * LANES : (c + 1) * LANES].reshape(senders, block, LANES)
            arrived[c, me] = packed[c, me]
        weights = mixw[...]
        weighted[...] = sel * (first * weights[0:1, :] + second * weights[1:2, :])
        earlier_at[...] = earlier

        def count_copy(d):
            return remote(cnt_send, cnt_all.at[me], cs_sem.at[d - 1], cr_sem.at[d - 1], peer(d), m)

        def block_copy(c, d):
            return remote(
                packed.at[c, peer(d)], arrived.at[c, me], as_sem.at[c, d - 1], ar_sem.at[c, d - 1], peer(d), m
            )

        def sibling_copy(c):
            return remote(xbuf.at[0, c], xbuf.at[1, c], ss_sem.at[0, c], sr_sem.at[0, c], me, sibling)

        def across_copy(c):
            return remote(xbuf.at[0, c], xbuf.at[2, c], ys_sem.at[c], yr_sem.at[c], me, across)

        def forward_copy(c):
            return remote(xbuf.at[2, c], xbuf.at[3, c], ss_sem.at[1, c], sr_sem.at[1, c], me, sibling)

        pl.semaphore_wait(barrier, senders - 1 + 3)
        for d in FAR_FIRST:
            count_copy(d).start()
        for c in range(chunks):
            for d in FAR_FIRST:
                block_copy(c, d).start()

        lane_e, lane_rest = split(iota_f((senders, stacked), 1), block)
        lane_g, lane_r = split(lane_rest[0:1, :], most)
        sender_at = iota_f((senders, stacked), 0)
        slot_j, slot_at = split(iota_f((STACK * n_slots, stacked), 0), n_slots)
        for d in range(1, senders):
            count_copy(d).wait_recv()
        counts = cnt_all[:, 0, :]
        lane_of = lax.broadcasted_iota(jnp.int32, (senders, LANES), 1)
        sender_of = lax.broadcasted_iota(jnp.int32, (senders, LANES), 0)
        mine = jnp.sum(jnp.where(lane_of == me, counts, 0.0), axis=1, keepdims=True)
        lane_cnt = jnp.sum(jnp.where(lane_e == sender_at, mine, 0.0), axis=0, keepdims=True)
        lane_off = jnp.sum(jnp.where(sender_at < lane_e, mine, 0.0), axis=0, keepdims=True)
        lane_slot = jnp.where(lane_r < lane_cnt, lane_off + lane_r, float(capacity))
        hit = flag(lane_slot == slot_at) * flag(lane_g == slot_j) * flag(slot_at < capacity)
        comp[...] = hit.astype(BF16)

        def prepare_return():
            spreader[...] = jnp.transpose(hit).astype(BF16)
            offset = jnp.sum(jnp.where(sender_of < me, counts, 0.0), axis=0, keepdims=True)
            of_row, _ = split(iota_f((stacked, LANES), 0), block)
            offset = jnp.sum(
                jnp.where(of_row == iota_f((stacked, LANES), 1), offset, 0.0), axis=1, keepdims=True
            )
            kept = weighted[...] * flag(offset + earlier_at[...] < capacity)
            high = kept.astype(BF16)
            low = (kept - high.astype(F32)).astype(BF16)
            _, token = split(iota_f((STACK * TOKEN_PAD, tok_rows), 0), TOKEN_PAD)
            spot = flag(token == iota_f((STACK * TOKEN_PAD, tok_rows), 1)).astype(BF16)
            seg, _ = split(iota_f((STACK * TOKEN_PAD, stacked), 0), TOKEN_PAD)
            there = flag(seg == lane_g)
            weigh[0] = (dot_nt(spot, high) * there).astype(BF16)
            weigh[1] = (dot_nt(spot, low) * there).astype(BF16)

        def take_chunk(c):
            for d in range(1, senders):
                block_copy(c, d).wait_recv()
            got = dot(comp[...], arrived[c].reshape(stacked, LANES)).astype(BF16)
            for j in range(STACK):
                xbuf[0, c, :, j * LANES : (j + 1) * LANES] = got[j * n_slots : (j + 1) * n_slots]
            across_copy(c).start()
            sibling_copy(c).start()

        prepare_return()
        for i, (which, c) in enumerate(passes):
            if which == 0:
                take_chunk(c)
            elif which == 1:
                sibling_copy(c).wait_recv()
            elif which == 2:
                across_copy(c).wait_recv()
                forward_copy(c).start()
            else:
                forward_copy(c).wait_recv()
            for up in range(2):
                for b in range(cols_of):
                    weight_copy(i, up, b).wait()
            x = xbuf[which, c]
            last = i == len(passes) - 1
            for b in range(cols_of):
                at = slice(b * SEG, (b + 1) * SEG)
                both = [dot(x, slots[2 * i + up, at, :]) for up in range(2)]
                if i:
                    both = [acc[up, :, at] + both[up] for up in range(2)]
                if last:
                    gate, up_act = both
                    hidden[:, at] = (gate / (1.0 + jnp.exp(-gate)) * up_act).astype(BF16)
                else:
                    acc[0, :, at], acc[1, :, at] = both
            for p in range(EXTRA + 2 * i, min(EXTRA + 2 * i + 2, 4 * chunks)):
                piece_copy(p).start(priority=1)

        def pair_copy(c):
            return remote(pair_send.at[c], pair_recv.at[c], ps_sem.at[c], pr_sem.at[c], me, sibling)

        def cross_copy(c):
            return remote(cross_send.at[c], cross_recv.at[c], xs_sem.at[c], xr_sem.at[c], me, across)

        def return_copy(c, d):
            return remote(
                ret_send.at[c, peer(d)], ret_recv.at[c, me], ts_sem.at[c, d - 1], tr_sem.at[c, d - 1], peer(d), m
            )

        def piece(c, o):
            piece_copy(4 * c + o).wait()
            return dot(hidden[...], slots[piece_slot(4 * c + o)])

        def send_back(c):
            cross_copy(c).wait_recv()
            total = (own[c] + cross_recv[c].astype(F32)).astype(BF16)
            total = jnp.concatenate([total[:, j * LANES : (j + 1) * LANES] for j in range(STACK)], axis=0)
            ret_send[c] = dot(spreader[...], total).astype(BF16).reshape(senders, block, LANES)
            ret_recv[c, me] = ret_send[c, me]
            for d in FAR_FIRST:
                return_copy(c, d).start()

        for c in range(chunks):
            pair_send[c, 0] = piece(c, 0).astype(BF16)
            pair_send[c, 1] = piece(c, 1).astype(BF16)
            pair_copy(c).start()
            if c:
                send_back(c - 1)
            cross = piece(c, 2)
            own[c] = piece(c, 3)
            pair_copy(c).wait_recv()
            cross_send[c] = (cross + pair_recv[c, 0].astype(F32)).astype(BF16)
            cross_copy(c).start()
            own[c] = own[c] + pair_recv[c, 1].astype(F32)
        send_back(chunks - 1)

        for c in range(chunks):
            for d in range(1, senders):
                return_copy(c, d).wait_recv()
            rows = ret_recv[c].reshape(stacked, LANES)
            mixed = (dot(weigh[0], rows) + dot(weigh[1], rows)).astype(BF16)
            for j in range(STACK):
                at = c * SEG + j * LANES
                out[:, at : at + LANES] = mixed[j * TOKEN_PAD : j * TOKEN_PAD + tok_rows]

        for d in range(1, senders):
            count_copy(d).wait_send()
        for c in range(chunks):
            for d in range(1, senders):
                block_copy(c, d).wait_send()
                return_copy(c, d).wait_send()
            across_copy(c).wait_send()
            sibling_copy(c).wait_send()
            forward_copy(c).wait_send()
            pair_copy(c).wait_send()
            cross_copy(c).wait_send()

    dma = pltpu.SemaphoreType.DMA
    others = senders - 1
    pl.run_scoped(
        body,
        dma((slots.shape[0], cols_of)), dma((3,)),
        dma((others,)), dma((others,)),
        dma((chunks, others)), dma((chunks, others)),
        dma((2, chunks)), dma((2, chunks)),
        dma((chunks,)), dma((chunks,)),
        dma((chunks,)), dma((chunks,)),
        dma((chunks,)), dma((chunks,)),
        dma((chunks, others)), dma((chunks, others)),
    )


def local_fused(tokens, mix_weights, routes, w_gate, w_up, w_down):
    tok_rows, width = tokens.shape
    senders = lax.axis_size("expert")
    capacity = 5 * tok_rows * senders * TOP // (4 * EXPERTS)
    n_slots = -(-capacity // ROUND_TO) * ROUND_TO
    ff = w_gate.shape[2]
    chunks = width // SEG
    block = STACK * (tok_rows // 2)
    stacked = senders * block
    vmem = pl.BlockSpec(memory_space=pltpu.VMEM)
    hbm = pl.BlockSpec(memory_space=pl.ANY)
    return pl.pallas_call(
        functools.partial(exchange, senders, capacity),
        out_shape=jax.ShapeDtypeStruct((tok_rows, width), BF16),
        in_specs=[hbm] * 6,
        out_specs=vmem,
        scratch_shapes=[
            pltpu.VMEM((8 * chunks + EXTRA, ff, SEG), BF16),
            pltpu.VMEM((tok_rows, width), BF16),
            pltpu.VMEM((TOP, tok_rows), jnp.int32),
            pltpu.VMEM((TOP, tok_rows), F32),
            pltpu.VMEM((chunks, senders, block, LANES), BF16),
            pltpu.VMEM((chunks, senders, block, LANES), BF16),
            pltpu.VMEM((4, chunks, n_slots, SEG), BF16),
            pltpu.VMEM((2, n_slots, ff), F32),
            pltpu.VMEM((n_slots, ff), BF16),
            pltpu.VMEM((8, LANES), F32),
            pltpu.VMEM((senders, 8, LANES), F32),
            pltpu.VMEM((stacked, tok_rows), F32),
            pltpu.VMEM((stacked, tok_rows), F32),
            pltpu.VMEM((STACK * n_slots, stacked), BF16),
            pltpu.VMEM((stacked, STACK * n_slots), BF16),
            pltpu.VMEM((2, STACK * TOKEN_PAD, stacked), BF16),
            pltpu.VMEM((chunks, n_slots, SEG), F32),
            pltpu.VMEM((chunks, 2, n_slots, SEG), BF16),
            pltpu.VMEM((chunks, 2, n_slots, SEG), BF16),
            pltpu.VMEM((chunks, n_slots, SEG), BF16),
            pltpu.VMEM((chunks, n_slots, SEG), BF16),
            pltpu.VMEM((chunks, senders, block, LANES), BF16),
            pltpu.VMEM((chunks, senders, block, LANES), BF16),
        ],
        compiler_params=pltpu.CompilerParams(
            collective_id=0, has_side_effects=True, vmem_limit_bytes=67_043_328
        ),
    )(tokens, mix_weights.T, routes.T, w_gate, w_up, w_down)


def fits(tokens, w_gate):
    senders, ways = lax.axis_size("expert"), lax.axis_size("mp")
    tok_rows, width = tokens.shape
    depth, ff = w_gate.shape[1], w_gate.shape[2]
    return (
        senders == EXPERTS
        and ways == 4
        and tok_rows % 8 == 0
        and (STACK * (tok_rows // 2)) % 16 == 0
        and tok_rows <= TOKEN_PAD
        and depth == 4 * width
        and width % SEG == 0
        and ff == STACK * SEG
        and (8 * (width // SEG) + EXTRA) * ff * SEG * 2 <= 58_800_000
    )


def local_any(tokens, mix_weights, routes, w_gate, w_up, w_down):
    form = local_fused if fits(tokens, w_gate) else local
    return form(tokens, mix_weights, routes, w_gate, w_up, w_down)


def pack_rows(pick_tokens, features, repeats):
    packed = jnp.einsum(
        "tem,tc->emc", pick_tokens, features, preferred_element_type=jnp.float32
    ).astype(jnp.bfloat16)
    spread = jnp.broadcast_to(packed[:, None], (packed.shape[0], repeats) + packed.shape[1:])
    return spread.reshape((packed.shape[0] * repeats,) + packed.shape[1:])


def activate(gate_act, up_act):
    return (jax.nn.silu(gate_act) * up_act).astype(jnp.bfloat16)


def local(tokens, mix_weights, routes, w_gate, w_up, w_down):
    tok_rows = tokens.shape[0]
    senders = lax.axis_size("expert")
    group_size = senders // EXPERTS
    capacity = 5 * tok_rows * senders * TOP // (4 * EXPERTS)
    most_rows = tok_rows // 2
    labels = jnp.arange(EXPERTS, dtype=jnp.int32)
    flat_ids = routes.reshape(-1)
    marked = (flat_ids[:, None] == labels[None, :]).astype(jnp.int32)
    earlier = jnp.cumsum(marked, axis=0) - marked
    local_rank = jnp.sum(earlier * marked, axis=1)
    counts = jnp.sum(marked, axis=0)
    count_grid = lax.all_gather(counts[None, :], "expert", axis=0, tiled=True)
    my_index = lax.axis_index("expert")
    sender_ids = jnp.arange(senders, dtype=jnp.int32)
    lower_mask = (sender_ids[:, None] < my_index).astype(jnp.int32)
    offsets = jnp.sum(count_grid * lower_mask, axis=0)
    slot_ids = jnp.sum(marked * offsets[None, :], axis=1) + local_rank
    keep_mask = (slot_ids < capacity).astype(jnp.int32)
    rank_hit = (local_rank[:, None] == jnp.arange(most_rows, dtype=jnp.int32)[None, :]).astype(
        jnp.int32
    ) * keep_mask[:, None]
    assign_pick = marked[:, :, None] * rank_hit[:, None, :]
    pick_tokens = jnp.sum(assign_pick.reshape(tok_rows, TOP, EXPERTS, most_rows), axis=1).astype(
        jnp.bfloat16
    )
    weighted = assign_pick.astype(jnp.float32) * mix_weights.reshape(-1)[:, None, None]
    combine_w = jnp.sum(weighted.reshape(tok_rows, TOP, EXPERTS * most_rows), axis=1)
    gate_rows = w_gate[0]
    up_rows = w_up[0]
    down_rows = w_down[0]
    arrived = lax.all_to_all(
        pack_rows(pick_tokens, tokens, group_size),
        "expert",
        split_axis=0,
        concat_axis=0,
        tiled=True,
    )
    arrived_rows = arrived.reshape(senders * most_rows, arrived.shape[2])
    shard_piece = lax.all_gather(arrived_rows, "mp", axis=1, tiled=True)
    gate_act = jnp.dot(shard_piece, gate_rows, preferred_element_type=jnp.float32)
    up_act = jnp.dot(shard_piece, up_rows, preferred_element_type=jnp.float32)
    hidden = activate(gate_act, up_act)
    part_sum = jnp.dot(hidden, down_rows, preferred_element_type=jnp.float32)
    reduced = lax.psum_scatter(part_sum, "mp", scatter_dimension=1, tiled=True).astype(jnp.bfloat16)
    out_width = reduced.shape[1]
    returned = lax.all_to_all(
        reduced.reshape(senders, most_rows, out_width),
        "expert",
        split_axis=0,
        concat_axis=0,
        tiled=True,
    )
    summed = jnp.sum(
        returned.reshape(EXPERTS, group_size, most_rows, out_width).astype(jnp.float32), axis=1
    )
    result = jnp.dot(
        combine_w, summed.reshape(EXPERTS * most_rows, out_width), precision=lax.Precision.HIGHEST
    )
    return result.astype(jnp.bfloat16)


def solution(mesh):
    placed = (
        P("expert", "mp"),
        P("expert", None),
        P("expert", None),
        P("expert", None, "mp"),
        P("expert", None, "mp"),
        P("expert", "mp", None),
    )
    return jax.shard_map(
        local_any, mesh=mesh, in_specs=placed, out_specs=P("expert", "mp"), check_vma=False
    )
```

time: 54.8 us -> 46.4 us (0.85)
  Pallas kernels: 50.3 us -> 44.8 us
  local copies, waits for them, and re-layouts: 4.23 us -> 1.52 us
    pallas_call x1, Pallas kernels: 50.3 us -> 44.8 us  [local_fused(): pl.pallas_call(functools.partial(exchange, senders, capacity), out_shape=...]
    unnamed x3 -> x1, local copies, waits for them, and re-layouts: 4.23 us -> 1.52 us
where the time goes in v1:
time: 46.4 us; the launch traced here: 46.3 us
  Pallas kernels  44.8 us (97%)
  local copies, waits for them, and re-layouts  1.52 us (3%)
    pallas_call x1, Pallas kernels, local_fused(): pl.pallas_call(functools.partial(exchange, senders, capacity), out_shape=...  44.8 us
    unnamed x1, local copies, waits for them, and re-layouts  1.52 us

profile of v1, /device:TPU:0, one launch (start us, length us, event | category | flops | bytes accessed | tf_op | source)
XLA Modules:
  0.0 46.3 jit_solution(5879556035064014415)
XLA Ops:
  0.0 44.8 %shard_map.64 = bf16[24,1536]{1,0:T(8,128)(2,1)} custom-call(bf16[24,1536]{1,0:T(8,128)(2,1)} %tokens.1, f32[2,24]{1,0:T(2,128)} %bitcast.2, s32[2,24]{1,0:T(2,128)} %bitcast.3, bf16[1,6144,2048]{2,1,0:T(8,128)(2,1)} %w_gate.1, bf16[1,6144,2048]{2,1,0:T(8,128)(2,1)} %w_up.1, bf16[1,2048,6144]{2,1,0:T(8,128)(2,1)} %w_down.1), custom_call_target="tpu_custom_call" | custom-call | tf_op jit(solution)/shard_map/pallas_call | solution.py:333
  44.8 1.5 %copy.8 = bf16[24,1536]{1,0:T(8,128)(2,1)} copy(bf16[24,1536]{1,0:T(8,128)(2,1)} %shard_map.64) | data formatting | bytes 147456

commit v2 on v1

--- a/solution.py
+++ b/solution.py
@@ -12,18 +12,48 @@
 STACK = 4
 LANES = 128
 SEG = STACK * LANES
+BACK = 2
+UNIT = BACK * LANES
 TOKEN_PAD = 32
-EXTRA = 4
+RING = 22
 ROUND_TO = 16
-FAR_FIRST = (4, 3, 5, 2, 6, 1, 7)
+FAR_FIRST = (7, 6, 5, 4, 3, 2, 1)
 MESH = pl.DeviceIdType.MESH
 BF16, F32 = jnp.bfloat16, jnp.float32
 
 
-def pass_order(chunks):
-    arrival = (0, 12, 34, 45)
-    pairs = [(which, c) for c in range(chunks) for which in range(4)]
-    return sorted(pairs, key=lambda p: 21 * p[1] + arrival[p[0]])
+def schedule(chunks):
+    last = chunks - 1
+    events = []
+    for c in range(last):
+        events += [("do", 0, c), ("wait", 0, c), ("group", (0, c))] + ([] if c else [("prepare",)])
+    events += [("do", 1, 0), ("do", 2, 0), ("do", 0, last)]
+    events += [("do", 1, c) for c in range(1, last)] + [("wait", 0, last), ("group", (0, last))]
+    events += [("do", 1, last)]
+    for c in range(chunks):
+        events += [("wait", 1, c)] + ([("do", 2, c + 1)] if c < last else [])
+        events += [("do", 3, c - 1)] if c else []
+        events += [("wait", 2, c), ("group", (1, c), (2, c))]
+    events += [("do", 3, last), *(("wait", 3, c) for c in range(last))]
+    events += [("group", *((3, c) for c in range(last)))]
+    events += [("wait", 3, last), ("group", (3, last))]
+    return events
+
+
+def down_order(units):
+    ahead = min(3, units)
+    order = [(0, u) for u in range(ahead)]
+    for u in range(units):
+        order += [(1, u)] + ([(0, u + ahead)] if u + ahead < units else [])
+    return order
+
+
+def piece_order(chunks):
+    first_use = {}
+    for half, unit in down_order(2 * chunks):
+        for owner in (2 * half, 2 * half + 1):
+            first_use.setdefault((owner, unit // 2), None)
+    return list(first_use)
 
 
 def dot(a, b):
@@ -56,12 +86,18 @@
 ):
     tok_rows, width = tokens.shape
     ff = w_gate.shape[2]
-    chunks, cols_of = width // SEG, ff // SEG
+    chunks, cols_of, units = width // SEG, ff // SEG, width // UNIT
     most = tok_rows // 2
     block = STACK * most
     stacked = senders * block
+    back_block = BACK * most
+    back_rows = senders * back_block
     n_slots = xbuf.shape[2]
-    passes = pass_order(chunks)
+    events = schedule(chunks)
+    passes = [part for event in events if event[0] == "group" for part in event[1:]]
+    pieces = piece_order(chunks)
+    ring = slots.shape[0]
+    loads = 2 * len(passes) + len(pieces)
 
     def body(
         w_sem, in_sem, cs_sem, cr_sem, as_sem, ar_sem, ss_sem, sr_sem, ys_sem, yr_sem,
@@ -72,11 +108,16 @@
         sibling = m + 1 - 2 * lax.rem(m, 2)
         across = lax.rem(m + 2, 4)
         across_sibling = lax.rem(sibling + 2, 4)
-        order = (m, sibling, across, across_sibling)
-        owners = (across_sibling, sibling, across, m)
+        odd = lax.rem(m, 2)
+        base = m - odd
+        sources = (base + 1, base, lax.rem(base + 3, 4), lax.rem(base + 2, 4))
+        held_at = (1 - odd, odd, 3 - odd, 2 + odd)
+        owners = (across_sibling, across, sibling, m)
+
+        bits = (lax.rem(me, 2), lax.rem(me // 2, 2), me // 4)
 
         def peer(d):
-            return lax.rem(me + d, senders)
+            return sum((1 - bit if d >> i & 1 else bit) * (1 << i) for i, bit in enumerate(bits))
 
         def remote(src, dst, send, recv, to_expert, to_mp):
             return pltpu.make_async_remote_copy(
@@ -84,48 +125,51 @@
                 device_id=(to_expert, to_mp), device_id_type=MESH,
             )
 
-        def weight_copy(i, up, b):
-            which, c = passes[i]
-            src = w_up if up else w_gate
-            start = pl.multiple_of(order[which] * width + c * SEG, SEG)
-            return pltpu.make_async_copy(
-                src.at[0, pl.ds(start, SEG), pl.ds(b * SEG, SEG)],
-                slots.at[2 * i + up, pl.ds(b * SEG, SEG), :],
-                w_sem.at[2 * i + up, b],
-            )
-
-        def piece_slot(p):
-            return 2 * len(passes) + p if p < EXTRA else p - EXTRA
-
-        def piece_copy(p):
-            start = pl.multiple_of(owners[p % 4] * width + (p // 4) * SEG, SEG)
-            return pltpu.make_async_copy(
-                w_down.at[0, :, pl.ds(start, SEG)], slots.at[piece_slot(p)], w_sem.at[piece_slot(p), 0]
-            )
-
+        def copies(k):
+            if k >= 2 * len(passes):
+                owner, c = pieces[k - 2 * len(passes)]
+                start = pl.multiple_of(owners[owner] * width + c * SEG, SEG)
+                return [pltpu.make_async_copy(w_down.at[0, :, pl.ds(start, SEG)], slots.at[k % ring], w_sem.at[k % ring, 0])]
+            source, c = passes[k // 2]
+            src = w_up if k % 2 else w_gate
+            start = pl.multiple_of(sources[source] * width + c * SEG, SEG)
+            return [
+                pltpu.make_async_copy(
+                    src.at[0, pl.ds(start, SEG), pl.ds(b * SEG, SEG)],
+                    slots.at[k % ring, pl.ds(b * SEG, SEG), :],
+                    w_sem.at[k % ring, b],
+                )
+                for b in range(cols_of)
+            ]
+
+        def fetch(k):
+            if k < loads:
+                for copy in copies(k):
+                    copy.start(priority=1)
+
+        def fetched(k):
+            for copy in copies(k):
+                copy.wait()
+
+        small = (
+            pltpu.make_async_copy(routes, ids, in_sem.at[0]),
+            pltpu.make_async_copy(tokens, tok, in_sem.at[1]),
+            pltpu.make_async_copy(mix, mixw, in_sem.at[2]),
+        )
+        for copy in small:
+            copy.start()
         barrier = pltpu.get_barrier_semaphore()
         for d in FAR_FIRST:
             pl.semaphore_signal(barrier, inc=1, device_id=(peer(d), m), device_id_type=MESH)
         for to in (across, across_sibling, sibling):
             pl.semaphore_signal(barrier, inc=1, device_id=(me, to), device_id_type=MESH)
-        loads = (
-            pltpu.make_async_copy(routes, ids, in_sem.at[0]),
-            pltpu.make_async_copy(tokens, tok, in_sem.at[1]),
-            pltpu.make_async_copy(mix, mixw, in_sem.at[2]),
-        )
-        for copy in loads:
-            copy.start()
-        for i in range(len(passes)):
-            for up in range(2):
-                for b in range(cols_of):
-                    weight_copy(i, up, b).start(priority=1)
-        for p in range(EXTRA):
-            piece_copy(p).start(priority=1)
+        for k in range(ring):
+            fetch(k)
 
         row_e, row_rest = split(iota_f((stacked, tok_rows), 0), block)
         row_g, row_r = split(row_rest, most)
         upper = flag(iota_f((tok_rows, tok_rows), 0) < iota_f((tok_rows, tok_rows), 1)).astype(BF16)
-        loads[0].wait()
+        small[0].wait()
         id_f = ids[...].astype(F32)
         first, second = flag(id_f[0:1, :] == row_e), flag(id_f[1:2, :] == row_e)
         marked = first + second
@@ -135,8 +179,8 @@
         named = (flag(id_f[0:1, :] == named) + flag(id_f[1:2, :] == named)).astype(BF16)
         cnt_send[...] = dot_nt(jnp.ones((8, tok_rows), BF16), named)
         cnt_all[me] = cnt_send[...]
-        loads[1].wait()
-        loads[2].wait()
+        small[1].wait()
+        small[2].wait()
         total = None
         for j in range(STACK):
             segs = [tok[:, c * SEG + j * LANES : c * SEG + (j + 1) * LANES] for c in range(chunks)]
@@ -174,35 +218,46 @@
             for d in FAR_FIRST:
                 block_copy(c, d).start()
 
-        lane_e, lane_rest = split(iota_f((senders, stacked), 1), block)
-        lane_g, lane_r = split(lane_rest[0:1, :], most)
-        sender_at = iota_f((senders, stacked), 0)
-        slot_j, slot_at = split(iota_f((STACK * n_slots, stacked), 0), n_slots)
         for d in range(1, senders):
             count_copy(d).wait_recv()
         counts = cnt_all[:, 0, :]
         lane_of = lax.broadcasted_iota(jnp.int32, (senders, LANES), 1)
         sender_of = lax.broadcasted_iota(jnp.int32, (senders, LANES), 0)
         mine = jnp.sum(jnp.where(lane_of == me, counts, 0.0), axis=1, keepdims=True)
-        lane_cnt = jnp.sum(jnp.where(lane_e == sender_at, mine, 0.0), axis=0, keepdims=True)
-        lane_off = jnp.sum(jnp.where(sender_at < lane_e, mine, 0.0), axis=0, keepdims=True)
-        lane_slot = jnp.where(lane_r < lane_cnt, lane_off + lane_r, float(capacity))
-        hit = flag(lane_slot == slot_at) * flag(lane_g == slot_j) * flag(slot_at < capacity)
-        comp[...] = hit.astype(BF16)
+
+        def placed(stack):
+            count = senders * stack * most
+            lane_e, lane_rest = split(iota_f((senders, count), 1), stack * most)
+            lane_g, lane_r = split(lane_rest[0:1, :], most)
+            sender_at = iota_f((senders, count), 0)
+            lane_cnt = jnp.sum(jnp.where(lane_e == sender_at, mine, 0.0), axis=0, keepdims=True)
+            lane_off = jnp.sum(jnp.where(sender_at < lane_e, mine, 0.0), axis=0, keepdims=True)
+            lane_slot = jnp.where(lane_r < lane_cnt, lane_off + lane_r, float(capacity))
+            slot_j, slot_at = split(iota_f((stack * n_slots, count), 0), n_slots)
+            hit = flag(lane_slot == slot_at) * flag(lane_g == slot_j) * flag(slot_at < capacity)
+            return hit.astype(BF16), lane_g
+
+        comp[...] = placed(STACK)[0]
 
         def prepare_return():
-            spreader[...] = jnp.transpose(hit).astype(BF16)
+            hit, lane_g = placed(BACK)
+            eye = flag(iota_f((back_rows, back_rows), 0) == iota_f((back_rows, back_rows), 1))
+            spreader[...] = dot_nt(eye.astype(BF16), hit).astype(BF16)
             offset = jnp.sum(jnp.where(sender_of < me, counts, 0.0), axis=0, keepdims=True)
-            of_row, _ = split(iota_f((stacked, LANES), 0), block)
+            of_row, _ = split(iota_f((back_rows, LANES), 0), back_block)
             offset = jnp.sum(
-                jnp.where(of_row == iota_f((stacked, LANES), 1), offset, 0.0), axis=1, keepdims=True
+                jnp.where(of_row == iota_f((back_rows, LANES), 1), offset, 0.0), axis=1, keepdims=True
             )
-            kept = weighted[...] * flag(offset + earlier_at[...] < capacity)
+            whole, ahead = (
+                at[...].reshape(senders, block, tok_rows)[:, :back_block].reshape(back_rows, tok_rows)
+                for at in (weighted, earlier_at)
+            )
+            kept = whole * flag(offset + ahead < capacity)
             high = kept.astype(BF16)
             low = (kept - high.astype(F32)).astype(BF16)
-            _, token = split(iota_f((STACK * TOKEN_PAD, tok_rows), 0), TOKEN_PAD)
-            spot = flag(token == iota_f((STACK * TOKEN_PAD, tok_rows), 1)).astype(BF16)
-            seg, _ = split(iota_f((STACK * TOKEN_PAD, stacked), 0), TOKEN_PAD)
+            _, token = split(iota_f((BACK * TOKEN_PAD, tok_rows), 0), TOKEN_PAD)
+            spot = flag(token == iota_f((BACK * TOKEN_PAD, tok_rows), 1)).astype(BF16)
+            seg, _ = split(iota_f((BACK * TOKEN_PAD, back_rows), 0), TOKEN_PAD)
             there = flag(seg == lane_g)
             weigh[0] = (dot_nt(spot, high) * there).astype(BF16)
             weigh[1] = (dot_nt(spot, low) * there).astype(BF16)
@@ -216,37 +271,52 @@
             across_copy(c).start()
             sibling_copy(c).start()
 
-        prepare_return()
-        for i, (which, c) in enumerate(passes):
-            if which == 0:
+        def do(source, c):
+            if source < 2:
                 take_chunk(c)
-            elif which == 1:
-                sibling_copy(c).wait_recv()
-            elif which == 2:
+            else:
                 across_copy(c).wait_recv()
                 forward_copy(c).start()
-            else:
-                forward_copy(c).wait_recv()
-            for up in range(2):
-                for b in range(cols_of):
-                    weight_copy(i, up, b).wait()
-            x = xbuf[which, c]
-            last = i == len(passes) - 1
+
+        def wait(source, c):
+            (sibling_copy if source < 2 else forward_copy)(c).wait_recv()
+
+        def group(parts, start, first, last):
+            for k in range(2 * start, 2 * (start + len(parts))):
+                fetched(k)
+            xs = [xbuf[held_at[source], c] for source, c in parts]
             for b in range(cols_of):
                 at = slice(b * SEG, (b + 1) * SEG)
-                both = [dot(x, slots[2 * i + up, at, :]) for up in range(2)]
-                if i:
+                both = [
+                    sum(dot(x, slots[(2 * (start + i) + up) % ring, at, :]) for i, x in enumerate(xs)) for up in range(2)
+                ]
+                if not first:
                     both = [acc[up, :, at] + both[up] for up in range(2)]
                 if last:
                     gate, up_act = both
                     hidden[:, at] = (gate / (1.0 + jnp.exp(-gate)) * up_act).astype(BF16)
                 else:
                     acc[0, :, at], acc[1, :, at] = both
-            for p in range(EXTRA + 2 * i, min(EXTRA + 2 * i + 2, 4 * chunks)):
-                piece_copy(p).start(priority=1)
-
-        def pair_copy(c):
-            return remote(pair_send.at[c], pair_recv.at[c], ps_sem.at[c], pr_sem.at[c], me, sibling)
+            for k in range(2 * start, 2 * (start + len(parts))):
+                fetch(k + ring)
+
+        done = 0
+        for event in events:
+            if event[0] == "prepare":
+                prepare_return()
+            elif event[0] == "group":
+                parts = event[1:]
+                group(parts, done, done == 0, done + len(parts) == len(passes))
+                done += len(parts)
+            else:
+                kind, source, c = event
+                acts = odd == (1 - source % 2 if kind == "do" else source % 2)
+                pl.when(acts)(functools.partial(do if kind == "do" else wait, source, c))
+
+        def pair_copy(o, c):
+            return remote(
+                pair_send.at[o, c], pair_recv.at[o, c], ps_sem.at[o, c], pr_sem.at[o, c], me, sibling
+            )
 
         def cross_copy(c):
             return remote(cross_send.at[c], cross_recv.at[c], xs_sem.at[c], xr_sem.at[c], me, across)
@@ -256,40 +326,53 @@
                 ret_send.at[c, peer(d)], ret_recv.at[c, me], ts_sem.at[c, d - 1], tr_sem.at[c, d - 1], peer(d), m
             )
 
-        def piece(c, o):
-            piece_copy(4 * c + o).wait()
-            return dot(hidden[...], slots[piece_slot(4 * c + o)])
+        def down_block(half, u):
+            at = [2 * len(passes) + pieces.index((2 * half + i, u // 2)) for i in range(2)]
+            if u % 2 == 0:
+                for k in at:
+                    fetched(k)
+            cols = slice(u % 2 * UNIT, (u % 2 + 1) * UNIT)
+            return [dot(hidden[...], slots[k % ring, :, cols]) for k in at]
+
+        def cross_step(c):
+            pair_copy(0, c).wait_recv()
+            cross_send[c] = (own[0, c] + pair_recv[0, c].astype(F32)).astype(BF16)
+            cross_copy(c).start()
 
         def send_back(c):
+            pair_copy(1, c).wait_recv()
             cross_copy(c).wait_recv()
-            total = (own[c] + cross_recv[c].astype(F32)).astype(BF16)
-            total = jnp.concatenate([total[:, j * LANES : (j + 1) * LANES] for j in range(STACK)], axis=0)
-            ret_send[c] = dot(spreader[...], total).astype(BF16).reshape(senders, block, LANES)
+            total = own[1, c] + pair_recv[1, c].astype(F32) + cross_recv[c].astype(F32)
+            total = total.astype(BF16)
+            total = jnp.concatenate([total[:, j * LANES : (j + 1) * LANES] for j in range(BACK)], axis=0)
+            ret_send[c] = dot(spreader[...], total).reshape(senders, back_block, LANES).astype(BF16)
             ret_recv[c, me] = ret_send[c, me]
             for d in FAR_FIRST:
                 return_copy(c, d).start()
 
-        for c in range(chunks):
-            pair_send[c, 0] = piece(c, 0).astype(BF16)
-            pair_send[c, 1] = piece(c, 1).astype(BF16)
-            pair_copy(c).start()
-            if c:
-                send_back(c - 1)
-            cross = piece(c, 2)
-            own[c] = piece(c, 3)
-            pair_copy(c).wait_recv()
-            cross_send[c] = (cross + pair_recv[c, 0].astype(F32)).astype(BF16)
-            cross_copy(c).start()
-            own[c] = own[c] + pair_recv[c, 1].astype(F32)
-        send_back(chunks - 1)
-
-        for c in range(chunks):
+        order = down_order(units)
+        crossing = {order.index((0, u)) + 2: u for u in range(units)}
+        returning = {}
+        for u in range(units):
+            returning.setdefault(min(max(order.index((0, u)) + 7, order.index((1, u)) + 2), len(order)), []).append(u)
+        for i, (half, u) in enumerate(order):
+            there, own[half, u] = down_block(half, u)
+            pair_send[half, u] = there.astype(BF16)
+            pair_copy(half, u).start()
+            if i in crossing:
+                cross_step(crossing[i])
+            for back in returning.get(i, ()):
+                send_back(back)
+        for back in returning.get(len(order), ()):
+            send_back(back)
+
+        for u in range(units):
             for d in range(1, senders):
-                return_copy(c, d).wait_recv()
-            rows = ret_recv[c].reshape(stacked, LANES)
+                return_copy(u, d).wait_recv()
+            rows = ret_recv[u].astype(F32).reshape(back_rows, LANES).astype(BF16)
             mixed = (dot(weigh[0], rows) + dot(weigh[1], rows)).astype(BF16)
-            for j in range(STACK):
-                at = c * SEG + j * LANES
+            for j in range(BACK):
+                at = u * UNIT + j * LANES
                 out[:, at : at + LANES] = mixed[j * TOKEN_PAD : j * TOKEN_PAD + tok_rows]
 
         for d in range(1, senders):
@@ -297,12 +380,15 @@
         for c in range(chunks):
             for d in range(1, senders):
                 block_copy(c, d).wait_send()
-                return_copy(c, d).wait_send()
             across_copy(c).wait_send()
             sibling_copy(c).wait_send()
             forward_copy(c).wait_send()
-            pair_copy(c).wait_send()
-            cross_copy(c).wait_send()
+        for u in range(units):
+            for d in range(1, senders):
+                return_copy(u, d).wait_send()
+            pair_copy(0, u).wait_send()
+            pair_copy(1, u).wait_send()
+            cross_copy(u).wait_send()
 
     dma = pltpu.SemaphoreType.DMA
     others = senders - 1
@@ -313,9 +399,9 @@
         dma((chunks, others)), dma((chunks, others)),
         dma((2, chunks)), dma((2, chunks)),
         dma((chunks,)), dma((chunks,)),
-        dma((chunks,)), dma((chunks,)),
-        dma((chunks,)), dma((chunks,)),
-        dma((chunks, others)), dma((chunks, others)),
+        dma((2, units)), dma((2, units)),
+        dma((units,)), dma((units,)),
+        dma((units, others)), dma((units, others)),
     )
 
 
@@ -328,15 +414,16 @@
     chunks = width // SEG
     block = STACK * (tok_rows // 2)
     stacked = senders * block
+    units, back_rows = width // UNIT, senders * BACK * (tok_rows // 2)
     vmem = pl.BlockSpec(memory_space=pltpu.VMEM)
-    hbm = pl.BlockSpec(memory_space=pl.ANY)
+    hbm = pl.BlockSpec(memory_space=pltpu.HBM)
     return pl.pallas_call(
         functools.partial(exchange, senders, capacity),
         out_shape=jax.ShapeDtypeStruct((tok_rows, width), BF16),
         in_specs=[hbm] * 6,
         out_specs=vmem,
         scratch_shapes=[
-            pltpu.VMEM((8 * chunks + EXTRA, ff, SEG), BF16),
+            pltpu.VMEM((RING, ff, SEG), BF16),
             pltpu.VMEM((tok_rows, width), BF16),
             pltpu.VMEM((TOP, tok_rows), jnp.int32),
             pltpu.VMEM((TOP, tok_rows), F32),
@@ -350,20 +437,20 @@
             pltpu.VMEM((stacked, tok_rows), F32),
             pltpu.VMEM((stacked, tok_rows), F32),
             pltpu.VMEM((STACK * n_slots, stacked), BF16),
-            pltpu.VMEM((stacked, STACK * n_slots), BF16),
-            pltpu.VMEM((2, STACK * TOKEN_PAD, stacked), BF16),
-            pltpu.VMEM((chunks, n_slots, SEG), F32),
-            pltpu.VMEM((chunks, 2, n_slots, SEG), BF16),
-            pltpu.VMEM((chunks, 2, n_slots, SEG), BF16),
-            pltpu.VMEM((chunks, n_slots, SEG), BF16),
-            pltpu.VMEM((chunks, n_slots, SEG), BF16),
-            pltpu.VMEM((chunks, senders, block, LANES), BF16),
-            pltpu.VMEM((chunks, senders, block, LANES), BF16),
+            pltpu.VMEM((back_rows, BACK * n_slots), BF16),
+            pltpu.VMEM((2, BACK * TOKEN_PAD, back_rows), BF16),
+            pltpu.VMEM((2, units, n_slots, UNIT), F32),
+            pltpu.VMEM((2, units, n_slots, UNIT), BF16),
+            pltpu.VMEM((2, units, n_slots, UNIT), BF16),
+            pltpu.VMEM((units, n_slots, UNIT), BF16),
+            pltpu.VMEM((units, n_slots, UNIT), BF16),
+            pltpu.VMEM((units, senders, back_rows // senders, LANES), BF16),
+            pltpu.VMEM((units, senders, back_rows // senders, LANES), BF16),
         ],
         compiler_params=pltpu.CompilerParams(
-            collective_id=0, has_side_effects=True, vmem_limit_bytes=67_043_328
+            collective_id=0, has_side_effects=True, vmem_limit_bytes=54_000_000
         ),
-    )(tokens, mix_weights.T, routes.T, w_gate, w_up, w_down)
+    )(*(pltpu.with_memory_space_constraint(a, pltpu.HBM) for a in (tokens, mix_weights.T, routes.T, w_gate, w_up, w_down)))
 
 
 def fits(tokens, w_gate):
@@ -375,11 +462,13 @@
         and ways == 4
         and tok_rows % 8 == 0
         and (STACK * (tok_rows // 2)) % 16 == 0
+        and (BACK * (tok_rows // 2)) % 8 == 0
         and tok_rows <= TOKEN_PAD
         and depth == 4 * width
         and width % SEG == 0
         and ff == STACK * SEG
-        and (8 * (width // SEG) + EXTRA) * ff * SEG * 2 <= 58_800_000
+        and width // SEG > 1
+        and RING * ff * SEG * 2 <= 47_000_000
     )
 
 

time: 46.4 us -> 37.5 us (0.81)
  Pallas kernels: 44.8 us -> 36.7 us
  local copies, waits for them, and re-layouts: 1.52 us -> 0.64 us
    pallas_call x1, Pallas kernels: 44.8 us -> 36.7 us  [local_fused(): pl.pallas_call(functools.partial(exchange, senders, capacity), out_shape=...]
    unnamed x1, local copies, waits for them, and re-layouts: 1.52 us -> 0.64 us
where the time goes in v2:
time: 37.5 us; the launch traced here: 37.4 us
  Pallas kernels  36.7 us (98%)
  local copies, waits for them, and re-layouts  0.64 us (2%)
    pallas_call x1, Pallas kernels, local_fused(): pl.pallas_call(functools.partial(exchange, senders, capacity), out_shape=...  36.7 us

profile of v2, /device:TPU:0, one launch (start us, length us, event | category | flops | bytes accessed | tf_op | source)
XLA Modules:
  0.0 37.4 jit_solution(14077814562015769859)
XLA Ops:
  0.0 36.7 %shard_map.64 = bf16[24,1536]{1,0:T(8,128)(2,1)S(1)} custom-call(bf16[24,1536]{1,0:T(8,128)(2,1)} %tokens.1, f32[2,24]{1,0:T(2,128)} %bitcast.2, s32[2,24]{1,0:T(2,128)} %bitcast.3, bf16[1,6144,2048]{2,1,0:T(8,128)(2,1)} %w_gate.1, bf16[1,6144,2048]{2,1,0:T(8,128)(2,1)} %w_up.1, bf16[1,2048,6144]{2,1,0:T(8,128)(2,1)} %w_down.1), custom_call_target="tpu_custom_call" | custom-call | tf_op jit(solution)/shard_map/pallas_call | solution.py:420
  36.7 0.6 %copy.8 = bf16[24,1536]{1,0:T(8,128)(2,1)} copy(bf16[24,1536]{1,0:T(8,128)(2,1)S(1)} %shard_map.64) | data formatting | bytes 147456
